TPU v7x, 512 devices: a whole 4x8x8 slice. The times are simulated.
512 devices in a mesh: group: 2 (over core), dp: 64 (over y, x, z_hi), mp: 4 (over z_lo).
Axes of the slice: x: 4, y: 8, z: 8 (z_hi: 2, z_lo: 4; z = z_hi * 4 + z_lo), core: 2. Of those that a mesh axis runs over, the one named last changes fastest.
Arguments:
- x_arrive: bfloat16 [256, 256, 1152], P(('group', 'dp')), may hold values from -6 to 6
- cond_first: int32 [128], P(('group', 'dp')), may hold values 0 or 1
- labels: int32 [128], P(('group', 'dp')), may hold values from 0 to 999
- step_ids: int32 [128], P(('group', 'dp')), may hold values from 0 to 999
- guidance: float32 [1], replicated, may hold values from 2 to 6
- time_table: bfloat16 [1000, 1152], P(None, 'mp'), may hold values from -6 to 6
- class_table: bfloat16 [1001, 1152], P(None, 'mp'), may hold values from -6 to 6
- ada_weight: bfloat16 [1152, 6912], P('mp', 'dp'), may hold values from -0.1875 to 0.1875
- final_ada: bfloat16 [1152, 2304], P('mp'), may hold values from -0.1875 to 0.1875
- qkv_weight: bfloat16 [3, 1152, 1152], P(None, 'dp', 'mp'), may hold values from -2 to 2
- proj_weight: bfloat16 [1152, 1152], P('mp', 'dp'), may hold values from -0.1875 to 0.1875
- fc1_weight: bfloat16 [1152, 4608], P('dp', 'mp'), may hold values from -0.1875 to 0.1875
- fc2_weight: bfloat16 [4608, 1152], P('mp', 'dp'), may hold values from -0.09375 to 0.09375
- out_weight: bfloat16 [1152, 16], replicated, may hold values from -0.1875 to 0.1875
Outputs:
- guided: float32 [128, 4096], P(('group', 'dp'), 'mp')
All inputs are finite; a program needn't handle non-finite values. No bound on the sum of `cond_first` on one device may be relied on, other than what follows from the above.
Results may differ from a plain program's by a relative error of at most 0.025.
Values may be sent and summed in bfloat16 or wider, within the bound.
No kernel may reach another device: no remote copies, remote signals or barrier semaphores. Data moves between devices by JAX's collectives and lax.ppermute only.
A program may use at most 64 MiB of HBM per device.

v0:
```python
import jax
import jax.numpy as jnp
from jax import lax
from jax.sharding import Mesh
from jax.sharding import PartitionSpec as P

HEADS = 16
CLASSES = 1000
DP = ("dp_0", "dp_1", "dp_2")
GROUP_DP = ("group", "dp_0", "dp_1", "dp_2")


def from_everyone(x, axis):
    size = lax.axis_size(axis)
    return lax.all_to_all(jnp.broadcast_to(x[None], (size, *x.shape)), axis, 0, 0, tiled=True)


def laid_out(pieces, dim):
    pieces = jnp.moveaxis(pieces, 0, dim)
    shape = pieces.shape
    return pieces.reshape(*shape[:dim], shape[dim] * shape[dim + 1], *shape[dim + 2 :])


def collect(x, axis, dim):
    pieces = from_everyone(x, axis)
    return laid_out(pieces, dim)


def of_everyone(x, axis):
    everything = from_everyone(x, axis)
    return jnp.sum(everything.astype(jnp.float32), axis=0)


def gathered_by_axis(x, axes, dim):
    for axis in reversed(axes):
        x = lax.all_gather(x, axis, axis=dim, tiled=True)
    return x


def cut_along(x, dim, size):
    shape = x.shape
    pieces = x.reshape(*shape[:dim], size, shape[dim] // size, *shape[dim + 1 :])
    return jnp.moveaxis(pieces, dim, 0)


def sum_at_owner(x, axis, dim):
    size = lax.axis_size(axis)
    pieces = lax.all_to_all(cut_along(x, dim, size), axis, 0, 0, tiled=True)
    return jnp.sum(pieces.astype(jnp.float32), axis=0)


def layer_norm(values):
    mean = jnp.mean(values, axis=-1, keepdims=True)
    centred = values - mean
    spread = jnp.mean(centred * centred, axis=-1, keepdims=True)
    return centred * lax.rsqrt(spread + 1e-06)


def on_device(
    x_arrive,
    cond_first,
    labels,
    step_ids,
    guidance,
    time_table,
    class_table,
    ada_weight,
    final_ada,
    qkv_weight,
    proj_weight,
    fc1_weight,
    fc2_weight,
    out_weight,
):
    pair_count = labels.shape[0]
    tokens = x_arrive.shape[1]
    width = x_arrive.shape[2]
    image_count = 2 * pair_count
    row_count = image_count * tokens
    split_rows = x_arrive.reshape(pair_count, 2, tokens, width)
    first = (cond_first == 1)[:, None, None]
    cond_rows = jnp.where(first, split_rows[:, 0], split_rows[:, 1])
    uncond_rows = jnp.where(first, split_rows[:, 1], split_rows[:, 0])
    x_sides = jnp.stack([cond_rows, uncond_rows])
    time_part = jnp.take(time_table, step_ids, axis=0).astype(jnp.float32)
    class_part = jnp.take(class_table, labels, axis=0).astype(jnp.float32)
    null_part = class_table[CLASSES].astype(jnp.float32)[None, :]
    emb_sides = time_part[None] + jnp.stack([class_part, null_part])
    act_sides = jax.nn.silu(emb_sides).astype(jnp.bfloat16)
    images, acts = (x_sides, act_sides)
    images = images.reshape(image_count, tokens, width)
    acts = acts.reshape(image_count, act_sides.shape[2])
    partial_final = jnp.dot(acts, final_ada, preferred_element_type=jnp.float32)
    every_act = collect(acts, DP, 0)
    column_part = jnp.dot(every_act, ada_weight, preferred_element_type=jnp.float32)
    summed, fmods = (
        of_everyone(column_part.astype(jnp.bfloat16), "mp").astype(jnp.float32),
        of_everyone(partial_final.astype(jnp.bfloat16), "mp").astype(jnp.float32),
    )
    mods = lax.all_to_all(
        summed.astype(jnp.bfloat16), DP, split_axis=0, concat_axis=1, tiled=True
    ).astype(summed.dtype)
    shift_a, scale_a, gate_a, shift_m, scale_m, gate_m = jnp.split(mods, 6, axis=1)
    shift_f, scale_f = jnp.split(fmods, 2, axis=1)
    images_f = images.astype(jnp.float32)
    hidden = (layer_norm(images_f) * (1.0 + scale_a[:, None]) + shift_a[:, None]).astype(
        jnp.bfloat16
    )
    hidden = hidden.reshape(row_count, width)
    quarter = qkv_weight.shape[2]
    head_dim = width // HEADS
    local_heads = quarter // head_dim
    columns = hidden
    qkv = jnp.einsum(
        "rd,kdc->krc",
        columns,
        lax.all_gather(qkv_weight, DP, axis=1, tiled=True),
        preferred_element_type=jnp.float32,
    ).astype(jnp.bfloat16)
    query = qkv[0].reshape(image_count, tokens, local_heads, head_dim)
    keys = qkv[1].reshape(image_count, tokens, local_heads, head_dim)
    values = qkv[2].reshape(image_count, tokens, local_heads, head_dim)
    scores = jnp.einsum(
        "bqhe,bkhe->bhqk", query, keys, preferred_element_type=jnp.float32
    ) * head_dim ** (-0.5)
    probs = jax.nn.softmax(scores, axis=-1).astype(jnp.bfloat16)
    mixed = jnp.einsum("bhqk,bkhe->bqhe", probs, values, preferred_element_type=jnp.float32).astype(
        jnp.bfloat16
    )
    mixed = mixed.reshape(row_count, quarter)
    attn_part = jnp.dot(mixed, collect(proj_weight, DP, 1), preferred_element_type=jnp.float32)
    attn = (
        lax.psum(attn_part.astype(jnp.bfloat16), "mp")
        .astype(jnp.float32)
        .reshape(image_count, tokens, width)
    )
    first_sum = images_f + gate_a[:, None] * attn
    hidden_two = (layer_norm(first_sum) * (1.0 + scale_m[:, None]) + shift_m[:, None]).astype(
        jnp.bfloat16
    )
    hidden_two = hidden_two.reshape(row_count, width)
    ff_quarter = fc1_weight.shape[1]
    columns = hidden_two
    up = jnp.dot(columns, gathered_by_axis(fc1_weight, DP, 0), preferred_element_type=jnp.float32)
    gelu_h = (
        jax.nn.gelu(up, approximate=True)
        .astype(jnp.bfloat16)
        .reshape(image_count, tokens, ff_quarter)
    )
    down_full = gathered_by_axis(fc2_weight, DP, 1)
    token_share = tokens // lax.axis_size("mp")
    mlp = sum_at_owner(
        jnp.einsum("btf,fd->tbd", gelu_h, down_full, preferred_element_type=jnp.float32).astype(
            jnp.bfloat16
        ),
        "mp",
        0,
    )
    token_start = lax.axis_index("mp") * token_share
    own_first = lax.dynamic_slice_in_dim(first_sum, token_start, token_share, 1).transpose(1, 0, 2)
    second_sum = own_first + gate_m[None] * mlp
    fin = (layer_norm(second_sum) * (1.0 + scale_f[None]) + shift_f[None]).astype(jnp.bfloat16)
    noise = jnp.einsum("tbd,do->bto", fin, out_weight, preferred_element_type=jnp.float32)
    noise = noise.reshape(2, pair_count, token_share * out_weight.shape[1])
    return noise[1] + guidance[0] * (noise[0] - noise[1])


def solution(mesh):
    torus = Mesh(
        mesh.devices.reshape(mesh.shape["group"], 8, 4, 2, mesh.shape["mp"]),
        ("group", "dp_0", "dp_1", "dp_2", "mp"),
    )
    placed = (
        P(GROUP_DP, None, None),
        P(GROUP_DP),
        P(GROUP_DP),
        P(GROUP_DP),
        P(),
        P(None, "mp"),
        P(None, "mp"),
        P("mp", DP),
        P("mp", None),
        P(None, DP, "mp"),
        P("mp", DP),
        P(DP, "mp"),
        P("mp", DP),
        P(),
    )
    return jax.shard_map(
        on_device, mesh=torus, in_specs=placed, out_specs=P(GROUP_DP, "mp"), check_vma=False
    )
```

profile of v0, /device:TPU:4, one launch (start us, length us, event | category | flops | bytes accessed | tf_op | source)
XLA Modules:
  0.0 341.8 jit_solution(6708045404015547400)
XLA Ops:
  13.9 19.2 %all-to-all-start = ((bf16[64,2,288]{2,1,0:T(2,128)(2,1)}), bf16[64,2,288]{2,1,0:T(2,128)(2,1)S(1)}, u32[]{:S(2)}, u32[]{:S(2)}) async-start(bf16[64,2,288]{2,1,0:T(2,128)(2,1)} %broadcast_in_dim.50), calls=%async_computation | async-start | bytes 196608 | tf_op jit(solution)/shard_map/all_to_all | solution.py:15
  33.8 12.4 %all-to-all-done = bf16[64,2,288]{2,1,0:T(2,128)(2,1)S(1)} async-done(((bf16[64,2,288]{2,1,0:T(2,128)(2,1)}), bf16[64,2,288]{2,1,0:T(2,128)(2,1)S(1)}, u32[]{:S(2)}, u32[]{:S(2)}) %all-to-all-start) | async-done | bytes 73760 | tf_op jit(solution)/shard_map/all_to_all | solution.py:15
  48.1 4.5 %all-to-all-start.1 = ((bf16[4,128,108]{1,2,0:T(8,128)(2,1)}), bf16[4,128,108]{1,2,0:T(8,128)(2,1)S(1)}, u32[]{:S(2)}, u32[]{:S(2)}) async-start(bf16[4,128,108]{1,2,0:T(8,128)(2,1)} %broadcast_in_dim.84), calls=%async_computation.1 | async-start | bytes 229376 | tf_op jit(solution)/shard_map/all_to_all | solution.py:15
  53.9 4.5 %all-to-all-done.1 = bf16[4,128,108]{1,2,0:T(8,128)(2,1)S(1)} async-done(((bf16[4,128,108]{1,2,0:T(8,128)(2,1)}), bf16[4,128,108]{1,2,0:T(8,128)(2,1)S(1)}, u32[]{:S(2)}, u32[]{:S(2)}) %all-to-all-start.1) | async-done | bytes 110624 | tf_op jit(solution)/shard_map/all_to_all | solution.py:15
  59.2 6.2 %all-to-all-start.2 = ((bf16[64,2,108]{2,1,0:T(2,128)(2,1)}), bf16[64,2,108]{2,1,0:T(2,128)(2,1)S(1)}, u32[]{:S(2)}, u32[]{:S(2)}) async-start(bf16[64,2,108]{2,1,0:T(2,128)(2,1)} %bitcast.7), calls=%async_computation.2 | async-start | bytes 65536 | tf_op jit(solution)/shard_map/all_to_all | solution.py:100
  65.6 12.4 %all-to-all-done.2 = bf16[64,2,108]{2,1,0:T(2,128)(2,1)S(1)} async-done(((bf16[64,2,108]{2,1,0:T(2,128)(2,1)}), bf16[64,2,108]{2,1,0:T(2,128)(2,1)S(1)}, u32[]{:S(2)}, u32[]{:S(2)}) %all-to-all-start.2) | async-done | bytes 27680 | tf_op jit(solution)/shard_map/all_to_all | solution.py:100
  79.1 7.2 %all-to-all-start.3 = ((bf16[64,288,18]{1,2,0:T(8,128)(2,1)}), bf16[64,288,18]{1,2,0:T(8,128)(2,1)}, u32[]{:S(2)}, u32[]{:S(2)}) async-start(bf16[64,288,18]{1,2,0:T(8,128)(2,1)} %broadcast_in_dim.85), calls=%async_computation.3 | async-start | bytes 2359296 | tf_op jit(solution)/shard_map/all_to_all | solution.py:15
  88.8 30.6 %all-to-all-done.3 = bf16[64,288,18]{1,2,0:T(8,128)(2,1)} async-done(((bf16[64,288,18]{1,2,0:T(8,128)(2,1)}), bf16[64,288,18]{1,2,0:T(8,128)(2,1)}, u32[]{:S(2)}, u32[]{:S(2)}) %all-to-all-start.3) | async-done | bytes 663584 | tf_op jit(solution)/shard_map/all_to_all | solution.py:15
  121.0 51.8 %all-gather.8.cloned.1.call-done = bf16[3,1152,288]{2,0,1:T(4,128)(2,1)} async-done(((bf16[3,18,288]{2,0,1:T(4,128)(2,1)}), bf16[3,1152,288]{2,0,1:T(4,128)(2,1)}) %all-gather.8.cloned.1.call-update) | async-done | bytes 1990672 | tf_op jit(solution)/shard_map/all_gather | solution.py:117
  172.8 3.7 %fusion.26 = bf16[3,512,288]{1,2,0:T(8,128)(2,1)S(1)} fusion(bf16[3,1152,288]{2,0,1:T(4,128)(2,1)} %all-gather.8.cloned.1.call-done, bf16[512,1152]{1,0:T(8,128)(2,1)} %fusion.16), kind=kOutput, calls=%fused_computation.41 | convolution fusion | flops 1019658240 | bytes 4055040 | tf_op jit(solution)/shard_map/rd,kdc->krc/dot_general | solution.py:114
  182.8 3.2 fusion.65
  186.0 2.0 fusion.30
  190.4 9.3 %all-gather = bf16[2,18,1152]{2,1,0:T(8,128)(2,1)S(1)} all-gather(bf16[1,18,1152]{2,1,0:T(8,128)(2,1)S(1)} %bitcast.125), channel_id=1, replica_groups=mesh['group'=2,'dp_0'=8,'dp_1'=4,'dp_2'=2,'mp'=4] {'dp_2'}, dimensions={0}, use_global_device_ids=true | all-gather | bytes 124416 | tf_op jit(solution)/shard_map/all_gather | solution.py:36
  199.8 11.3 %all-gather.1 = bf16[4,36,1152]{2,1,0:T(8,128)(2,1)S(1)} all-gather(bf16[1,36,1152]{2,1,0:T(8,128)(2,1)S(1)} %reshape.323), channel_id=1, replica_groups=mesh['group'=2,'dp_0'=8,'dp_1'=4,'dp_2'=2,'mp'=4] {'dp_1'}, dimensions={0}, use_global_device_ids=true | all-gather | bytes 414720 | tf_op jit(solution)/shard_map/all_gather | solution.py:36
  211.9 10.3 %all-gather.2 = bf16[2,18,1152]{2,1,0:T(8,128)(2,1)S(1)} all-gather(bf16[1,18,1152]{2,1,0:T(8,128)(2,1)S(1)} %bitcast.126), channel_id=1, replica_groups=mesh['group'=2,'dp_0'=8,'dp_1'=4,'dp_2'=2,'mp'=4] {'dp_2'}, dimensions={0}, use_global_device_ids=true | all-gather | bytes 124416 | tf_op jit(solution)/shard_map/all_gather | solution.py:36
  222.2 12.4 %all-gather.3 = bf16[4,36,1152]{2,1,0:T(8,128)(2,1)S(1)} all-gather(bf16[1,36,1152]{2,1,0:T(8,128)(2,1)S(1)} %reshape.327), channel_id=1, replica_groups=mesh['group'=2,'dp_0'=8,'dp_1'=4,'dp_2'=2,'mp'=4] {'dp_1'}, dimensions={0}, use_global_device_ids=true | all-gather | bytes 414720 | tf_op jit(solution)/shard_map/all_gather | solution.py:36
  236.5 3.4 %all-to-all-start.5 = ((bf16[4,2,2304]{2,1,0:T(2,128)(2,1)}), bf16[4,2,2304]{2,1,0:T(2,128)(2,1)S(1)}, u32[]{:S(2)}, u32[]{:S(2)}) async-start(bf16[4,2,2304]{2,1,0:T(2,128)(2,1)} %broadcast_in_dim.86), calls=%async_computation.5 | async-start | bytes 73728 | tf_op jit(solution)/shard_map/all_to_all | solution.py:15
  240.0 21.1 %all-reduce.2.cloned.1.call-done = bf16[512,1152]{1,0:T(8,128)(2,1)} async-done(((bf16[512,1152]{1,0:T(8,128)(2,1)}), bf16[512,1152]{1,0:T(8,128)(2,1)}) %all-reduce.2.cloned.1.call-update) | async-done | bytes 1179664 | tf_op jit(solution)/shard_map/psum | solution.py:133
  264.9 2.0 fusion.12
  266.9 4.0 %fusion.11 = bf16[512,1152]{1,0:T(8,128)(2,1)S(1)} fusion(bf16[512,1152]{1,0:T(8,128)(2,1)} %fusion.12, bf16[1152,1152]{1,0:T(8,128)(2,1)} %all-gather.10.cloned.1.call-done), kind=kOutput, calls=%fused_computation.15 | convolution fusion | flops 1364262912 | bytes 5013504 | tf_op jit(solution)/shard_map/dot_general | solution.py:144
  271.0 25.5 %all-gather.12.cloned.1.call-done = bf16[1152,1152]{0,1:T(8,128)(2,1)} async-done(((bf16[1152,144]{0,1:T(8,128)(2,1)}), bf16[1152,1152]{0,1:T(8,128)(2,1)}) %all-gather.12.cloned.1.call-update) | async-done | bytes 2654224 | tf_op jit(solution)/shard_map/all_gather | solution.py:36
  296.4 3.6 %convolution_convert_fusion.1 = bf16[2,256,1152]{2,1,0:T(8,128)(2,1)S(1)} fusion(bf16[2,256,1152]{2,1,0:T(8,128)(2,1)S(1)} %bitcast.131, bf16[1152,1152]{0,1:T(8,128)(2,1)} %all-gather.12.cloned.1.call-done), kind=kOutput, calls=%fused_computation.3 | convolution fusion | flops 1359544320 | bytes 5013504 | tf_op jit(solution)/shard_map/btf,fd->tbd/dot_general | solution.py:153
  301.2 4.8 %all-to-all-start.4 = ((bf16[4,64,2,1152]{3,1,2,0:T(8,128)(2,1)}), bf16[4,64,2,1152]{3,1,2,0:T(8,128)(2,1)S(1)}, u32[]{:S(2)}, u32[]{:S(2)}) async-start(bf16[4,64,2,1152]{3,1,2,0:T(8,128)(2,1)} %copy.113), calls=%async_computation.4 | async-start | bytes 2359296 | tf_op jit(solution)/shard_map/all_to_all | solution.py:48
  306.7 24.8 %all-to-all-done.4 = bf16[4,64,2,1152]{3,1,2,0:T(8,128)(2,1)S(1)} async-done(((bf16[4,64,2,1152]{3,1,2,0:T(8,128)(2,1)}), bf16[4,64,2,1152]{3,1,2,0:T(8,128)(2,1)S(1)}, u32[]{:S(2)}, u32[]{:S(2)}) %all-to-all-start.4) | async-done | bytes 1179680 | tf_op jit(solution)/shard_map/all_to_all | solution.py:48
  (91 shorter events, 33.7 us)
Async XLA Ops:
  7.4 228.2 %copy-start = (bf16[288,2304]{1,0:T(8,128)(2,1)S(1)}, bf16[288,2304]{1,0:T(8,128)(2,1)}, u32[]{:S(2)}) copy-start(bf16[288,2304]{1,0:T(8,128)(2,1)} %param.22) | copy-start | bytes 3981316
  7.4 165.5 %all-gather.8.cloned.1.call-start = ((), (), s32[]{:S(2)}) async-start(), calls=%async_computation.6 | async-start | bytes 3594240 | tf_op jit(solution)/shard_map/all_gather | solution.py:117
  12.7 0.6 copy-start.6
  13.9 64.1 %copy-start.5 = (bf16[288,18]{0,1:T(8,128)(2,1)S(1)}, bf16[288,18]{0,1:T(8,128)(2,1)}, u32[]{:S(2)}) copy-start(bf16[288,18]{0,1:T(8,128)(2,1)} %param.24) | copy-start | bytes 31108
  13.9 32.3 %all-to-all-start = ((bf16[64,2,288]{2,1,0:T(2,128)(2,1)}), bf16[64,2,288]{2,1,0:T(2,128)(2,1)S(1)}, u32[]{:S(2)}, u32[]{:S(2)}) async-start(bf16[64,2,288]{2,1,0:T(2,128)(2,1)} %broadcast_in_dim.50), calls=%async_computation | async-start | bytes 196608 | tf_op jit(solution)/shard_map/all_to_all | solution.py:15
  48.1 10.4 %all-to-all-start.1 = ((bf16[4,128,108]{1,2,0:T(8,128)(2,1)}), bf16[4,128,108]{1,2,0:T(8,128)(2,1)S(1)}, u32[]{:S(2)}, u32[]{:S(2)}) async-start(bf16[4,128,108]{1,2,0:T(8,128)(2,1)} %broadcast_in_dim.84), calls=%async_computation.1 | async-start | bytes 229376 | tf_op jit(solution)/shard_map/all_to_all | solution.py:15
  59.2 18.8 %all-to-all-start.2 = ((bf16[64,2,108]{2,1,0:T(2,128)(2,1)}), bf16[64,2,108]{2,1,0:T(2,128)(2,1)S(1)}, u32[]{:S(2)}, u32[]{:S(2)}) async-start(bf16[64,2,108]{2,1,0:T(2,128)(2,1)} %bitcast.7), calls=%async_computation.2 | async-start | bytes 65536 | tf_op jit(solution)/shard_map/all_to_all | solution.py:100
  79.1 40.3 %all-to-all-start.3 = ((bf16[64,288,18]{1,2,0:T(8,128)(2,1)}), bf16[64,288,18]{1,2,0:T(8,128)(2,1)}, u32[]{:S(2)}, u32[]{:S(2)}) async-start(bf16[64,288,18]{1,2,0:T(8,128)(2,1)} %broadcast_in_dim.85), calls=%async_computation.3 | async-start | bytes 2359296 | tf_op jit(solution)/shard_map/all_to_all | solution.py:15
  86.3 174.8 %all-reduce.2.cloned.1.call-start = ((), (), s32[]{:S(2)}) async-start(), calls=%async_computation.7 | async-start | bytes 2359296 | tf_op jit(solution)/shard_map/psum | solution.py:133
  188.0 2.4 copy-start.3
  188.4 23.6 %copy-start.4 = (bf16[1152,18]{0,1:T(8,128)(2,1)S(1)}, bf16[1152,18]{0,1:T(8,128)(2,1)}, u32[]{:S(2)}) copy-start(bf16[1152,18]{0,1:T(8,128)(2,1)} %param.26) | copy-start | bytes 124420
  190.3 45.2 %copy-start.7 = (bf16[2,288]{1,0:T(2,128)(2,1)S(1)}, bf16[2,288]{1,0:T(2,128)(2,1)}, u32[]{:S(2)}) copy-start(bf16[2,288]{1,0:T(2,128)(2,1)} %copy-done.6) | copy-start | bytes 3460
  190.4 76.6 %all-gather.10.cloned.1.call-start = ((), (), s32[]{:S(2)}) async-start(), calls=%async_computation.8 | async-start | bytes 2985984 | tf_op jit(solution)/shard_map/all_gather | solution.py:36
  211.9 84.6 %all-gather.12.cloned.1.call-start = ((), (), s32[]{:S(2)}) async-start(), calls=%async_computation.9 | async-start | bytes 2985984 | tf_op jit(solution)/shard_map/all_gather | solution.py:36
  236.5 64.7 %all-to-all-start.5 = ((bf16[4,2,2304]{2,1,0:T(2,128)(2,1)}), bf16[4,2,2304]{2,1,0:T(2,128)(2,1)S(1)}, u32[]{:S(2)}, u32[]{:S(2)}) async-start(bf16[4,2,2304]{2,1,0:T(2,128)(2,1)} %broadcast_in_dim.86), calls=%async_computation.5 | async-start | bytes 73728 | tf_op jit(solution)/shard_map/all_to_all | solution.py:15
  262.8 1.4 copy-start.1
  262.8 2.1 copy-start.2
  301.2 30.3 %all-to-all-start.4 = ((bf16[4,64,2,1152]{3,1,2,0:T(8,128)(2,1)}), bf16[4,64,2,1152]{3,1,2,0:T(8,128)(2,1)S(1)}, u32[]{:S(2)}, u32[]{:S(2)}) async-start(bf16[4,64,2,1152]{3,1,2,0:T(8,128)(2,1)} %copy.113), calls=%async_computation.4 | async-start | bytes 2359296 | tf_op jit(solution)/shard_map/all_to_all | solution.py:48
  305.9 27.1 %copy-start.8 = (bf16[1152,16]{0,1:T(8,128)(2,1)S(1)}, bf16[1152,16]{0,1:T(8,128)(2,1)}, u32[]{:S(2)}) copy-start(bf16[1152,16]{0,1:T(8,128)(2,1)} %param.27) | copy-start | bytes 110596
Sparse Core Ops, SparseCore 0:
  12.5 160.2 all-gather.7
  190.5 70.5 all-reduce.1
Sparse Core Ops, SparseCore 1:
  212.0 38.8 all-gather.9
  252.8 43.6 all-gather.11
where the time goes:
time: 343 us; the launch traced here: 342 us
  waiting for transfers between devices  183 us (53%)
  starting transfers between devices  45.4 us (13%)
  blocking collectives  43.3 us (13%)
  local copies, waits for them, and re-layouts  21.6 us (6%)
  matrix products  20.2 us (6%)
  between operations  17.8 us (5%)
  other arithmetic  10.3 us (3%)
    all_gather x1, waiting for transfers between devices, on_device(): lax.all_gather(qkv_weight, DP, axis=1, tiled=True)  51.8 us
    all_to_all x4, waiting for transfers between devices, from_everyone(): lax.all_to_all(jnp.broadcast_to(x[None], (size, *x.shape)), axis, 0, 0, t...  47.6 us
    all_gather x4, blocking collectives, gathered_by_axis(): x = lax.all_gather(x, axis, axis=dim, tiled=True)  43.3 us
    all_to_all x4, starting transfers between devices, from_everyone(): lax.all_to_all(jnp.broadcast_to(x[None], (size, *x.shape)), axis, 0, 0, t...  34.3 us
    all_gather x2, waiting for transfers between devices, gathered_by_axis(): x = lax.all_gather(x, axis, axis=dim, tiled=True)  25.5 us
    all_to_all x1, waiting for transfers between devices, sum_at_owner(): pieces = lax.all_to_all(cut_along(x, dim, size), axis, 0, 0, tiled=True)  24.8 us
    psum x1, waiting for transfers between devices, on_device(): lax.psum(attn_part.astype(jnp.bfloat16), 'mp').astype(jnp.float32)  21.1 us
    all_to_all x1, waiting for transfers between devices, on_device(): lax.all_to_all(summed.astype(jnp.bfloat16), DP, split_axis=0, concat_axis...  12.4 us
  transfers between devices with their start and end apart: 10, of which 8 were waited for; matrix products, arithmetic and copies ran while one was open for 8% of the time, Pallas kernels for 0%

commit v1 on v0

--- a/solution.py
+++ b/solution.py
@@ -8,6 +8,9 @@
 CLASSES = 1000
 DP = ("dp_0", "dp_1", "dp_2")
 GROUP_DP = ("group", "dp_0", "dp_1", "dp_2")
+store_skins = lambda mesh_ax, packet: jnp.concatenate(
+    lax.all_to_all(jnp.stack(lax.axis_size(mesh_ax) * [packet]), mesh_ax, 0, 0), 1
+)
 
 
 def from_everyone(x, axis):
@@ -112,10 +115,7 @@
     local_heads = quarter // head_dim
     columns = hidden
     qkv = jnp.einsum(
-        "rd,kdc->krc",
-        columns,
-        lax.all_gather(qkv_weight, DP, axis=1, tiled=True),
-        preferred_element_type=jnp.float32,
+        "rd,kdc->krc", columns, store_skins(DP, qkv_weight), preferred_element_type=jnp.float32
     ).astype(jnp.bfloat16)
     query = qkv[0].reshape(image_count, tokens, local_heads, head_dim)
     keys = qkv[1].reshape(image_count, tokens, local_heads, head_dim)

time: 343 us -> 388 us (1.13)
  blocking collectives: 43.3 us -> 142 us
  waiting for transfers between devices: 183 us -> 150 us
  starting transfers between devices: 45.4 us -> 17.2 us
  local copies, waits for them, and re-layouts: 21.6 us -> 29.8 us
    all_to_all x0 -> x4, blocking collectives: none -> 96.9 us  [the longest x3 78.7 us: from_everyone(): lax.all_to_all(jnp.broadcast_to(x[None], (size, *x.shape)), axis, 0, 0, t...]
    all_to_all x1, waiting for transfers between devices: 12.4 us -> 77.5 us  [lax.all_to_all(jnp.stack(lax.axis_size(mesh_ax) * [packet]), mesh_ax, 0, 0)]
    all_gather x1 -> x0, waiting for transfers between devices: 51.8 us -> none  [on_device(): lax.all_gather(qkv_weight, DP, axis=1, tiled=True)]
    all_to_all x4 -> x1, waiting for transfers between devices: 47.6 us -> 0.01 us  [from_everyone(): lax.all_to_all(jnp.broadcast_to(x[None], (size, *x.shape)), axis, 0, 0, t...]
    all_to_all x4 -> x1, starting transfers between devices: 34.3 us -> 4.27 us  [from_everyone(): lax.all_to_all(jnp.broadcast_to(x[None], (size, *x.shape)), axis, 0, 0, t...]
    reshape x0 -> x2, local copies, waits for them, and re-layouts: none -> 9.83 us  [jnp.concatenate(lax.all_to_all(jnp.stack(lax.axis_size(mesh_ax) * [packet...]
  transfers between devices with their start and end apart: 10 -> 6, of which waited for: 8 -> 4; matrix products, arithmetic and copies ran while one was open for 8% -> 5% of each run, Pallas kernels for 0% -> 0%
where the time goes in v1:
time: 388 us; the launch traced here: 386 us
  waiting for transfers between devices  150 us (39%)
  blocking collectives  142 us (37%)
  local copies, waits for them, and re-layouts  29.8 us (8%)
  matrix products  19.9 us (5%)
  between operations  17.9 us (5%)
  starting transfers between devices  17.2 us (4%)
  other arithmetic  10.1 us (3%)
    all_to_all x3, blocking collectives, from_everyone(): lax.all_to_all(jnp.broadcast_to(x[None], (size, *x.shape)), axis, 0, 0, t...  78.7 us
    all_to_all x1, waiting for transfers between devices, lax.all_to_all(jnp.stack(lax.axis_size(mesh_ax) * [packet]), mesh_ax, 0, 0)  77.5 us
    all_gather x4, blocking collectives, gathered_by_axis(): x = lax.all_gather(x, axis, axis=dim, tiled=True)  44.9 us
    all_gather x2, waiting for transfers between devices, gathered_by_axis(): x = lax.all_gather(x, axis, axis=dim, tiled=True)  26.3 us
    all_to_all x1, waiting for transfers between devices, sum_at_owner(): pieces = lax.all_to_all(cut_along(x, dim, size), axis, 0, 0, tiled=True)  24.8 us
    psum x1, waiting for transfers between devices, on_device(): lax.psum(attn_part.astype(jnp.bfloat16), 'mp').astype(jnp.float32)  21 us
    all_to_all x1, blocking collectives, on_device(): lax.all_to_all(summed.astype(jnp.bfloat16), DP, split_axis=0, concat_axis...  18.2 us
    reshape x2, local copies, waits for them, and re-layouts, jnp.concatenate(lax.all_to_all(jnp.stack(lax.axis_size(mesh_ax) * [packet...  9.83 us
  transfers between devices with their start and end apart: 6, of which 4 were waited for; matrix products, arithmetic and copies ran while one was open for 5% of the time, Pallas kernels for 0%

profile of v1, /device:TPU:4, one launch (start us, length us, event | category | flops | bytes accessed | tf_op | source)
XLA Modules:
  0.0 386.3 jit_solution(8923832303763434914)
XLA Ops:
  11.8 32.0 %all_to_all.43 = bf16[64,2,288]{2,1,0:T(2,128)(2,1)S(1)} all-to-all(bf16[64,2,288]{2,1,0:T(2,128)(2,1)S(1)} %broadcast_in_dim.50), channel_id=1, replica_groups=mesh['group'=2,'dp_0'=8,'dp_1'=4,'dp_2'=2,'mp'=4] {'dp_0','dp_1','dp_2'}, dimensions={0} | all-to-all | bytes 147456 | tf_op jit(solution)/shard_map/all_to_all | solution.py:18
  45.0 10.2 %all_to_all.44 = bf16[4,128,108]{1,2,0:T(8,128)(2,1)S(1)} all-to-all(bf16[4,128,108]{1,2,0:T(8,128)(2,1)S(1)} %broadcast_in_dim.84), channel_id=1, replica_groups=mesh['group'=2,'dp_0'=8,'dp_1'=4,'dp_2'=2,'mp'=4] {'mp'}, dimensions={0} | all-to-all | bytes 221184 | tf_op jit(solution)/shard_map/all_to_all | solution.py:18
  55.3 18.2 %all_to_all.45 = bf16[64,2,108]{2,1,0:T(2,128)(2,1)S(1)} all-to-all(bf16[64,2,108]{2,1,0:T(2,128)(2,1)S(1)} %bitcast.116), channel_id=1, replica_groups=mesh['group'=2,'dp_0'=8,'dp_1'=4,'dp_2'=2,'mp'=4] {'dp_0','dp_1','dp_2'}, dimensions={0} | all-to-all | bytes 55296 | tf_op jit(solution)/shard_map/all_to_all | solution.py:103
  74.3 36.5 %all_to_all.46 = bf16[64,288,18]{1,2,0:T(8,128)(2,1)} all-to-all(bf16[64,288,18]{1,2,0:T(8,128)(2,1)S(1)} %broadcast_in_dim.85), channel_id=1, replica_groups=mesh['group'=2,'dp_0'=8,'dp_1'=4,'dp_2'=2,'mp'=4] {'dp_0','dp_1','dp_2'}, dimensions={0} | all-to-all | bytes 1327104 | tf_op jit(solution)/shard_map/all_to_all | solution.py:18
  110.9 2.1 stack.11
  113.0 7.8 %all-to-all-start.3 = ((bf16[64,3,18,288]{3,2,1,0:T(8,128)(2,1)}), bf16[64,3,18,288]{3,2,1,0:T(8,128)(2,1)}, u32[]{:S(2)}, u32[]{:S(2)}) async-start(bf16[64,3,18,288]{3,2,1,0:T(8,128)(2,1)} %stack.11), calls=%async_computation.3 | async-start | bytes 7077888 | tf_op jit(solution)/shard_map/all_to_all | solution.py:12
  126.9 77.5 %all-to-all-done.3 = bf16[64,3,18,288]{3,2,1,0:T(8,128)(2,1)} async-done(((bf16[64,3,18,288]{3,2,1,0:T(8,128)(2,1)}), bf16[64,3,18,288]{3,2,1,0:T(8,128)(2,1)}, u32[]{:S(2)}, u32[]{:S(2)}) %all-to-all-start.3) | async-done | bytes 1990688 | tf_op jit(solution)/shard_map/all_to_all | solution.py:12
  204.4 4.2 %copy.109 = bf16[3,64,18,288]{3,2,1,0:T(8,128)(2,1)} copy(bf16[3,64,18,288]{3,2,0,1:T(8,128)(2,1)} %bitcast.11) | data formatting | bytes 3981312 | tf_op jit(solution)/shard_map/reshape | solution.py:11
  208.6 5.7 %reshape.324 = bf16[3,1152,288]{2,1,0:T(8,128)(2,1)} reshape(bf16[3,64,18,288]{3,2,1,0:T(8,128)(2,1)} %copy.109) | data formatting | bytes 3981312 | tf_op jit(solution)/shard_map/reshape | solution.py:11
  214.3 3.5 fusion.21
  224.0 3.2 fusion.55
  227.2 2.0 fusion.22
  231.8 8.7 %all-gather = bf16[2,18,1152]{2,1,0:T(8,128)(2,1)S(1)} all-gather(bf16[1,18,1152]{2,1,0:T(8,128)(2,1)S(1)} %bitcast.117), channel_id=1, replica_groups=mesh['group'=2,'dp_0'=8,'dp_1'=4,'dp_2'=2,'mp'=4] {'dp_2'}, dimensions={0}, use_global_device_ids=true | all-gather | bytes 124416 | tf_op jit(solution)/shard_map/all_gather | solution.py:39
  240.6 13.4 %all-gather.1 = bf16[4,36,1152]{2,1,0:T(8,128)(2,1)S(1)} all-gather(bf16[1,36,1152]{2,1,0:T(8,128)(2,1)S(1)} %reshape.387), channel_id=1, replica_groups=mesh['group'=2,'dp_0'=8,'dp_1'=4,'dp_2'=2,'mp'=4] {'dp_1'}, dimensions={0}, use_global_device_ids=true | all-gather | bytes 414720 | tf_op jit(solution)/shard_map/all_gather | solution.py:39
  254.9 10.3 %all-gather.2 = bf16[2,18,1152]{2,1,0:T(8,128)(2,1)S(1)} all-gather(bf16[1,18,1152]{2,1,0:T(8,128)(2,1)S(1)} %bitcast.118), channel_id=1, replica_groups=mesh['group'=2,'dp_0'=8,'dp_1'=4,'dp_2'=2,'mp'=4] {'dp_2'}, dimensions={0}, use_global_device_ids=true | all-gather | bytes 124416 | tf_op jit(solution)/shard_map/all_gather | solution.py:39
  265.2 12.4 %all-gather.3 = bf16[4,36,1152]{2,1,0:T(8,128)(2,1)S(1)} all-gather(bf16[1,36,1152]{2,1,0:T(8,128)(2,1)S(1)} %reshape.391), channel_id=1, replica_groups=mesh['group'=2,'dp_0'=8,'dp_1'=4,'dp_2'=2,'mp'=4] {'dp_1'}, dimensions={0}, use_global_device_ids=true | all-gather | bytes 414720 | tf_op jit(solution)/shard_map/all_gather | solution.py:39
  279.4 4.3 %all-to-all-start.6 = ((bf16[4,2,2304]{2,1,0:T(2,128)(2,1)}), bf16[4,2,2304]{2,1,0:T(2,128)(2,1)S(1)}, u32[]{:S(2)}, u32[]{:S(2)}) async-start(bf16[4,2,2304]{2,1,0:T(2,128)(2,1)} %broadcast_in_dim.86), calls=%async_computation.6 | async-start | bytes 73728 | tf_op jit(solution)/shard_map/all_to_all | solution.py:18
  283.7 21.0 %all-reduce.2.cloned.1.call-done = bf16[512,1152]{1,0:T(8,128)(2,1)} async-done(((bf16[512,1152]{1,0:T(8,128)(2,1)}), bf16[512,1152]{1,0:T(8,128)(2,1)}) %all-reduce.2.cloned.1.call-update) | async-done | bytes 1179664 | tf_op jit(solution)/shard_map/psum | solution.py:133
  308.6 2.0 fusion.10
  310.6 4.0 %fusion.9 = bf16[512,1152]{1,0:T(8,128)(2,1)S(1)} fusion(bf16[512,1152]{1,0:T(8,128)(2,1)} %fusion.10, bf16[1152,1152]{1,0:T(8,128)(2,1)} %all-gather.7.cloned.1.call-done), kind=kOutput, calls=%fused_computation.13 | convolution fusion | flops 1364262912 | bytes 5013504 | tf_op jit(solution)/shard_map/dot_general | solution.py:144
  314.6 26.3 %all-gather.9.cloned.1.call-done = bf16[1152,1152]{0,1:T(8,128)(2,1)} async-done(((bf16[1152,144]{0,1:T(8,128)(2,1)}), bf16[1152,1152]{0,1:T(8,128)(2,1)}) %all-gather.9.cloned.1.call-update) | async-done | bytes 2654224 | tf_op jit(solution)/shard_map/all_gather | solution.py:39
  340.9 3.6 convolution_convert_fusion.1
  345.6 4.8 %all-to-all-start.5 = ((bf16[4,64,2,1152]{3,1,2,0:T(8,128)(2,1)}), bf16[4,64,2,1152]{3,1,2,0:T(8,128)(2,1)S(1)}, u32[]{:S(2)}, u32[]{:S(2)}) async-start(bf16[4,64,2,1152]{3,1,2,0:T(8,128)(2,1)} %copy.116), calls=%async_computation.5 | async-start | bytes 2359296 | tf_op jit(solution)/shard_map/all_to_all | solution.py:51
  351.2 24.8 %all-to-all-done.5 = bf16[4,64,2,1152]{3,1,2,0:T(8,128)(2,1)S(1)} async-done(((bf16[4,64,2,1152]{3,1,2,0:T(8,128)(2,1)}), bf16[4,64,2,1152]{3,1,2,0:T(8,128)(2,1)S(1)}, u32[]{:S(2)}, u32[]{:S(2)}) %all-to-all-start.5) | async-done | bytes 1179680 | tf_op jit(solution)/shard_map/all_to_all | solution.py:51
  (86 shorter events, 29.9 us)
Async XLA Ops:
  7.4 271.1 %copy-start = (bf16[288,2304]{1,0:T(8,128)(2,1)S(1)}, bf16[288,2304]{1,0:T(8,128)(2,1)}, u32[]{:S(2)}) copy-start(bf16[288,2304]{1,0:T(8,128)(2,1)} %param.22) | copy-start | bytes 3981316
  11.2 0.6 copy-start.6
  11.8 99.1 %copy-start.5 = (bf16[3,18,288]{2,1,0:T(8,128)(2,1)S(1)}, bf16[3,18,288]{2,1,0:T(8,128)(2,1)}, u32[]{:S(2)}) copy-start(bf16[3,18,288]{2,1,0:T(8,128)(2,1)} %param.23) | copy-start | bytes 93316
  113.0 91.5 %all-to-all-start.3 = ((bf16[64,3,18,288]{3,2,1,0:T(8,128)(2,1)}), bf16[64,3,18,288]{3,2,1,0:T(8,128)(2,1)}, u32[]{:S(2)}, u32[]{:S(2)}) async-start(bf16[64,3,18,288]{3,2,1,0:T(8,128)(2,1)} %stack.11), calls=%async_computation.3 | async-start | bytes 7077888 | tf_op jit(solution)/shard_map/all_to_all | solution.py:12
  120.8 183.9 %all-reduce.2.cloned.1.call-start = ((), (), s32[]{:S(2)}) async-start(), calls=%async_computation.7 | async-start | bytes 2359296 | tf_op jit(solution)/shard_map/psum | solution.py:133
  229.2 2.6 copy-start.3
  229.6 25.2 %copy-start.4 = (bf16[1152,18]{0,1:T(8,128)(2,1)S(1)}, bf16[1152,18]{0,1:T(8,128)(2,1)}, u32[]{:S(2)}) copy-start(bf16[1152,18]{0,1:T(8,128)(2,1)} %param.26) | copy-start | bytes 124420
  231.6 47.0 %copy-start.7 = (bf16[2,288]{1,0:T(2,128)(2,1)S(1)}, bf16[2,288]{1,0:T(2,128)(2,1)}, u32[]{:S(2)}) copy-start(bf16[2,288]{1,0:T(2,128)(2,1)} %copy-done.6) | copy-start | bytes 3460
  231.6 79.0 %all-gather.7.cloned.1.call-start = ((), (), s32[]{:S(2)}) async-start(), calls=%async_computation.8 | async-start | bytes 2985984 | tf_op jit(solution)/shard_map/all_gather | solution.py:39
  254.8 86.1 %all-gather.9.cloned.1.call-start = ((), (), s32[]{:S(2)}) async-start(), calls=%async_computation.9 | async-start | bytes 2985984 | tf_op jit(solution)/shard_map/all_gather | solution.py:39
  279.4 66.2 %all-to-all-start.6 = ((bf16[4,2,2304]{2,1,0:T(2,128)(2,1)}), bf16[4,2,2304]{2,1,0:T(2,128)(2,1)S(1)}, u32[]{:S(2)}, u32[]{:S(2)}) async-start(bf16[4,2,2304]{2,1,0:T(2,128)(2,1)} %broadcast_in_dim.86), calls=%async_computation.6 | async-start | bytes 73728 | tf_op jit(solution)/shard_map/all_to_all | solution.py:18
  306.4 1.5 copy-start.1
  306.4 2.1 copy-start.2
  345.6 30.3 %all-to-all-start.5 = ((bf16[4,64,2,1152]{3,1,2,0:T(8,128)(2,1)}), bf16[4,64,2,1152]{3,1,2,0:T(8,128)(2,1)S(1)}, u32[]{:S(2)}, u32[]{:S(2)}) async-start(bf16[4,64,2,1152]{3,1,2,0:T(8,128)(2,1)} %copy.116), calls=%async_computation.5 | async-start | bytes 2359296 | tf_op jit(solution)/shard_map/all_to_all | solution.py:51
  350.4 27.1 %copy-start.8 = (bf16[1152,16]{0,1:T(8,128)(2,1)S(1)}, bf16[1152,16]{0,1:T(8,128)(2,1)}, u32[]{:S(2)}) copy-start(bf16[1152,16]{0,1:T(8,128)(2,1)} %param.27) | copy-start | bytes 110596
Sparse Core Ops, SparseCore 0:
  231.7 72.9 all-reduce.1
Sparse Core Ops, SparseCore 1:
  254.9 40.3 all-gather.6
  297.1 43.7 all-gather.8
